TPU v7x, 32 devices: a whole 2x2x4 slice. The times are simulated.
32 devices in a mesh: gx: 8 (over y, x, core), gy: 4 (over z).
Axes of the slice: x: 2, y: 2, z: 4, core: 2. Of those that a mesh axis runs over, the one named last changes fastest.
Arguments:
- cells: int32 [3, 1048576], P(None, ('gx', 'gy')), may hold values from 0 to 255, as said below
- fractions: float32 [3, 1048576], P(None, ('gx', 'gy')), may hold values from 0 to 1
- charges: float32 [1048576], P(('gx', 'gy')), may hold values from -24 to 24
- influence: float32 [256, 256, 256], P('gx', 'gy'), may hold values from 0.05 to 24, as said below
- shells: int32 [256, 256, 256], P('gx', 'gy'), may hold values from 0 to 255
Outputs:
- potential_hat: float32 [2, 256, 256, 256], P(None, 'gx', 'gy')
- energy: float32 [], replicated
- virial: float32 [3, 3], replicated
- spectrum: float32 [256], replicated
Inputs may be any that keep to these rules, and one draw needn't show every extreme that they name: `cells`: atom a belongs to device a // 32768, devices numbered with gy fastest; its y cell lies in that device's block of 32 y planes (block index its gx index) and its z cell in its block of 64 z planes (block index its gy index). `influence`: Positive.
All inputs are finite; a program needn't handle non-finite values.
Results may differ from a plain program's by a relative error of at most 0.0029.
Values sent between devices are 32-bit elements; how exact they have to be, the bound alone decides.
No kernel may reach another device: no remote copies, remote signals or barrier semaphores. Data moves between devices by JAX's collectives and lax.ppermute only.
A program may use at most 64 MiB of HBM per device.

v0:
```python
import math
import jax
import jax.numpy as jnp
from jax import lax
from jax.sharding import PartitionSpec as P

MESH = 256
SHELLS = 256
SCREEN = 4096


def passed_along(block, axis, distance):
    devices = range(lax.axis_size(axis))
    route = [((i - distance) % len(devices), i) for i in devices]
    return lax.ppermute(block, axis, route)


def spline(frac):
    cube = frac * frac * frac
    square = frac * frac
    rest = 1.0 - frac
    return (
        rest * rest * rest / 6.0,
        (3.0 * cube - 6.0 * square + 4.0) / 6.0,
        (-3.0 * cube + 3.0 * square + 3.0 * frac + 1.0) / 6.0,
        cube / 6.0,
    )


def place_weights(weights, target, columns, wrapped):
    result = jnp.zeros(columns.shape, jnp.float32)
    for offset in range(4):
        column = target[:, None] + offset
        if wrapped:
            column = column % MESH
        result = result + jnp.where(columns == column, weights[offset][:, None], 0.0)
    return result


def wave_tables():
    index = jnp.arange(MESH, dtype=jnp.int32)
    phase = index[:, None] * index[None, :] % MESH
    angle = phase.astype(jnp.float32) * (2.0 * math.pi / MESH)
    factor = 1.0 / math.sqrt(MESH)
    return (jnp.cos(angle) * factor, -jnp.sin(angle) * factor)


def wave_numbers(index):
    return jnp.where(index < MESH // 2, index, index - MESH).astype(jnp.float32)


def shards(cells, fractions, charges, influence, shells):
    rows_y = lax.axis_size("gx")
    cols_z = lax.axis_size("gy")
    plane_y = MESH // rows_y
    plane_z = MESH // cols_z
    first_y = lax.axis_index("gx") * plane_y
    first_z = lax.axis_index("gy") * plane_z
    ext_y = plane_y + 3
    ext_z = plane_z + 3
    count = charges.shape[0]
    block = min(2048, count)
    columns_x = lax.broadcasted_iota(jnp.int32, (block, MESH), 1)
    columns_y = lax.broadcasted_iota(jnp.int32, (block, ext_y), 1)
    columns_z = lax.broadcasted_iota(jnp.int32, (block, ext_z), 1)

    def spread(turn, accum):
        begin = turn * block
        cell = lax.dynamic_slice_in_dim(cells, begin, block, 1)
        frac = lax.dynamic_slice_in_dim(fractions, begin, block, 1)
        charge = lax.dynamic_slice_in_dim(charges, begin, block, 0)
        table_x = place_weights(spline(frac[0]), cell[0], columns_x, True)
        table_y = place_weights(spline(frac[1]), cell[1] - first_y, columns_y, False)
        wave_table_z = place_weights(spline(frac[2]), cell[2] - first_z, columns_z, False)
        factor_x = (charge[:, None] * table_x).astype(jnp.bfloat16)
        factor_yz = (
            (table_y[:, :, None] * wave_table_z[:, None, :])
            .reshape(block, ext_y * ext_z)
            .astype(jnp.bfloat16)
        )
        return accum + jnp.einsum(
            "ap,ax->px", factor_yz, factor_x, preferred_element_type=jnp.float32
        )

    spread_mesh = lax.fori_loop(
        0, count // block, spread, jnp.zeros((ext_y * ext_z, MESH), jnp.float32)
    )
    spread_mesh = spread_mesh.reshape(ext_y, ext_z, MESH)
    arrived = passed_along(spread_mesh[plane_y:], "gx", 1)
    spread_mesh = spread_mesh[:plane_y].at[:3].add(arrived)
    arrived_z = passed_along(spread_mesh[:, plane_z:], "gy", 1)
    spread_mesh = spread_mesh[:, :plane_z].at[:, :3].add(arrived_z)
    keep_y, keep_z = (plane_y, plane_z)
    cosine, minus_sine = wave_tables()
    real_table = jnp.stack([cosine, minus_sine])
    complex_table = jnp.stack([jnp.stack([cosine, -minus_sine]), jnp.stack([minus_sine, cosine])])
    upper_limit = lax.Precision.HIGHEST
    kx_rows = MESH // rows_y
    ky_rows = MESH // cols_z
    flat_mesh = spread_mesh.reshape(keep_y * keep_z, MESH)
    along_x = jnp.einsum("ckx,px->ckp", real_table, flat_mesh, precision=upper_limit)
    moved = lax.all_to_all(along_x[None], "gx", split_axis=2, concat_axis=0, tiled=True)
    moved = moved.reshape(rows_y, 2, kx_rows, keep_y, keep_z)
    table_y = complex_table.reshape(2, 2, MESH, rows_y, plane_y)
    along_y = jnp.einsum("ocKst,scktz->okKz", table_y, moved, precision=upper_limit)
    shifted_along_z = lax.all_to_all(
        along_y.reshape(2, kx_rows, MESH * keep_z)[None],
        "gy",
        split_axis=3,
        concat_axis=0,
        tiled=True,
    )
    shifted_along_z = shifted_along_z.reshape(cols_z, 2, kx_rows, ky_rows, keep_z)
    wave_table_z = complex_table.reshape(2, 2, MESH, cols_z, plane_z)
    structure_factor = jnp.einsum(
        "whzir,ihnqr->wnqz", wave_table_z, shifted_along_z, precision=upper_limit
    )
    wave_x = wave_numbers(lax.axis_index("gx") * kx_rows + jnp.arange(kx_rows, dtype=jnp.int32))[
        :, None, None
    ]
    wave_y = wave_numbers(lax.axis_index("gy") * ky_rows + jnp.arange(ky_rows, dtype=jnp.int32))[
        None, :, None
    ]
    wave_z = wave_numbers(jnp.arange(MESH, dtype=jnp.int32))[None, None, :]
    squared = wave_x * wave_x + wave_y * wave_y + wave_z * wave_z
    keep = jnp.where(squared > 0.0, 1.0, 0.0).astype(jnp.float32)
    weight = keep * influence
    potential_hat = structure_factor * weight[None]
    power = structure_factor[0] * structure_factor[0] + structure_factor[1] * structure_factor[1]
    influence_weighted = weight * power
    scale = 0.5 / MESH**3
    local_sum = jnp.sum(influence_weighted)
    coef = influence_weighted * 2.0 * (1.0 + squared / SCREEN) / (squared + 1.0 - keep)
    shape = coef.shape
    vectors = jnp.stack(
        [
            jnp.broadcast_to(wave_x, shape),
            jnp.broadcast_to(wave_y, shape),
            jnp.broadcast_to(wave_z, shape),
        ]
    )
    cross = jnp.einsum("akyz,bkyz->ab", vectors * coef[None], vectors, precision=upper_limit)
    virial_part = scale * (jnp.eye(3, dtype=jnp.float32) * local_sum - cross)
    energy_part = scale * local_sum
    shell_labels = jnp.arange(SHELLS, dtype=jnp.int32)

    def shell_rows(accum, pair):
        power_spectrum_row, shell_row = pair
        onehot = (shell_row.reshape(-1)[:, None] == shell_labels[None, :]).astype(jnp.float32)
        return (
            accum + jnp.dot(power_spectrum_row.reshape(-1), onehot, precision=upper_limit),
            None,
        )

    shell_sums, unused = lax.scan(shell_rows, jnp.zeros((SHELLS,), jnp.float32), (power, shells))
    spectrum_part = shell_sums * (SHELLS / MESH**3)
    energy, virial, spectrum = lax.psum((energy_part, virial_part, spectrum_part), ("gx", "gy"))
    return (potential_hat, energy, virial, spectrum)


def solution(mesh):
    return jax.shard_map(
        shards,
        mesh=mesh,
        in_specs=(
            P(None, ("gx", "gy")),
            P(None, ("gx", "gy")),
            P(("gx", "gy")),
            P("gx", "gy", None),
            P("gx", "gy", None),
        ),
        out_specs=(P(None, "gx", "gy", None), P(), P(), P()),
        check_vma=False,
    )
```

profile of v0, /device:TPU:14, one launch (start us, length us, event | category | flops | bytes accessed | tf_op | source)
XLA Modules:
  0.0 1131.8 jit_solution(5072555203006667526)
XLA Ops:
  0.6 474.0 %while.31 = (s32[]{:T(128)}, f32[2345,256]{1,0:T(8,128)S(1)}, s32[3,32768]{1,0:T(4,128)}, s32[]{:T(128)}, f32[3,32768]{1,0:T(4,128)}, /*index=5*/s32[]{:T(128)},...) while((s32[]{:T(128)}, f32[2345,256]{1,0:T(8,128)S(1)}, ...), condition=%wide.region_1.2_spmd.clone.clone, body=%wide.region_0.1_spmd.clone.clone.sunk | while | flops 2479059456 | bytes 45443312 | solution.py:85
  3.1 7.1 multiply_convert_fusion.6
  10.1 9.3 convert_element_type.169
  20.2 10.1 convolution_add_fusion.2
  32.7 7.1 multiply_convert_fusion.6
  39.8 9.3 convert_element_type.169
  49.8 10.1 convolution_add_fusion.2
  62.3 7.1 multiply_convert_fusion.6
  69.4 9.3 convert_element_type.169
  79.4 10.1 convolution_add_fusion.2
  91.9 7.1 multiply_convert_fusion.6
  99.0 9.3 convert_element_type.169
  109.0 10.1 convolution_add_fusion.2
  121.6 7.1 multiply_convert_fusion.6
  128.6 9.3 convert_element_type.169
  138.7 10.1 convolution_add_fusion.2
  151.2 7.1 multiply_convert_fusion.6
  158.3 9.3 convert_element_type.169
  168.3 10.1 convolution_add_fusion.2
  180.8 7.1 multiply_convert_fusion.6
  187.9 9.3 convert_element_type.169
  197.9 10.1 convolution_add_fusion.2
  210.4 7.1 multiply_convert_fusion.6
  217.5 9.3 convert_element_type.169
  227.5 10.1 convolution_add_fusion.2
  240.0 7.1 multiply_convert_fusion.6
  247.1 9.3 convert_element_type.169
  257.2 10.1 convolution_add_fusion.2
  269.7 7.1 multiply_convert_fusion.6
  276.8 9.3 convert_element_type.169
  286.8 10.1 convolution_add_fusion.2
  299.3 7.1 multiply_convert_fusion.6
  306.4 9.3 convert_element_type.169
  316.4 10.1 convolution_add_fusion.2
  328.9 7.1 multiply_convert_fusion.6
  336.0 9.3 convert_element_type.169
  346.0 10.1 convolution_add_fusion.2
  358.5 7.1 multiply_convert_fusion.6
  365.6 9.3 convert_element_type.169
  375.6 10.1 convolution_add_fusion.2
  388.2 7.1 multiply_convert_fusion.6
  395.2 9.3 convert_element_type.169
  405.3 10.1 convolution_add_fusion.2
  417.8 7.1 multiply_convert_fusion.6
  424.9 9.3 convert_element_type.169
  434.9 10.1 convolution_add_fusion.2
  447.4 7.1 multiply_convert_fusion.6
  454.5 9.3 convert_element_type.169
  464.5 10.1 convolution_add_fusion.2
  505.7 45.7 %all-to-all-done = f32[1,2,256,2048]{3,1,0,2:T(2,128)} async-done(((f32[1,2,256,2048]{3,1,0,2:T(2,128)}), f32[1,2,256,2048]{3,1,0,2:T(2,128)}, u32[]{:S(2)}, u32[]{:S(2)}) %all-to-all-start) | async-done | bytes 4194336 | tf_op jit(solution)/shard_map/all_to_all | solution.py:102
  551.4 8.0 copy.35
  559.4 7.9 reshape.1077
  567.2 17.7 %fusion.64 = f32[2,32,256,64]{2,3,0,1:T(8,128)} fusion(f32[8,2,32,32,64,1]{4,3,0,1,2,5:T(8,128)} %reshape.1077, f32[1,1,256,8,32]{2,4,3,1,0:T(8,128)S(1)} %get-tuple-element.478, f32[1,1,256,8,32]{2,4,3,1,0:T(8,128)S(1)} %get-tuple-element.477, f32[1,1,256,8,32]{2,4,3,1,0:T(8,128)S(1)} %get-tuple-element.476), kind=kOutput, calls=%fused_computation.123 | convolution fusion | flops 6443237376 | bytes 9175040 | tf_op jit(solution)/shard_map/ocKst,scktz->okKz/dot_general | solution.py:105
  584.9 15.2 %copy.26 = f32[2,32,256,64]{1,0,3,2:T(2,128)} copy(f32[2,32,256,64]{2,3,0,1:T(8,128)} %fusion.64) | data formatting | bytes 8388608 | tf_op jit(solution)/shard_map/broadcast_in_dim;reshape | solution.py:107
  600.1 19.4 %reshape.1087 = f32[4,1,262144]{2,1,0:T(1,128)} reshape(f32[16384,1,2,32]{3,2,1,0:T(2,128)} %bitcast.105) | data formatting | bytes 8388608
  627.7 88.8 %all-to-all-done.1 = f32[4,1,262144]{2,1,0:T(1,128)} async-done(((f32[4,1,262144]{2,1,0:T(1,128)}), f32[4,1,262144]{2,1,0:T(1,128)}, u32[]{:S(2)}, u32[]{:S(2)}) %all-to-all-start.1) | async-done | bytes 4194336 | tf_op jit(solution)/shard_map/all_to_all | solution.py:106
  717.0 15.5 %reduce.4 = f32[4,262144]{1,0:T(4,128)} reduce(f32[4,1,262144]{2,1,0:T(1,128)} %all-to-all-done.1, f32[]{:T(128)} %broadcast.1645), dimensions={1}, to_apply=%all_to_all.25.reduce_sub_computation | reduce | bytes 8388612 | tf_op jit(solution)/shard_map/all_to_all | solution.py:106
  732.5 26.8 %reshape.1088 = f32[16384,1,2,32]{3,2,1,0:T(2,128)} reshape(f32[4,262144]{1,0:T(4,128)} %reduce.4) | data formatting | bytes 8388608
  759.3 22.1 %copy.19 = f32[1,2,32,4,4096]{4,3,2,1,0:T(4,128)} copy(f32[1,2,32,4,4096]{2,1,4,3,0:T(2,128)} %bitcast.106) | data formatting | bytes 8388608 | tf_op jit(solution)/shard_map/all_to_all | solution.py:106
  781.3 8.1 reshape.1080
  789.5 9.5 fusion.59
  805.6 222.5 %while.30 = (s32[]{:T(128)}, f32[256]{0:T(256)S(1)}, f32[32,64,256]{2,1,0:T(8,128)}, s32[32,64,256]{2,1,0:T(8,128)}, s32[]{:T(128)}, /*index=5*/s32[]{:T(128)}) while((s32[]{:T(128)}, f32[256]{0:T(256)S(1)}, f32[32,64,256]{2,1,0:T(8,128)}, s32[32,64,256]{2,1,0:T(8,128)}, s32[]{:T(128)}, /*index=5*/s32[]{:T(128)}) %tuple.124), condition=%wide.region_6.7_spmd.clone, body=%wide.region_5.6_spmd.clone.sunk | while | flops 54526464 | bytes 659543 | solution.py:155
  1037.9 45.6 %fusion.82 = f32[3,3]{1,0:T(4,128)S(1)} fusion(f32[1,32,64,256]{3,0,2,1:T(1,128)} %stack_broadcast_in_dim.8, f32[1,32,64,256]{3,0,2,1:T(1,128)} %stack_broadcast_in_dim.7, f32[1,32,64,256]{3,0,2,1:T(1,128)} %stack_broadcast_in_dim.6, f32[32,64,256]{2,1,0:T(8,128)} %get-tuple-element.443, f32[]{:T(128)} %multiply_reduce_fusion), kind=kOutput, calls=%fused_computation.134 | convolution fusion | flops 64487460 | bytes 8388648 | tf_op jit(solution)/shard_map/akyz,bkyz->ab/dot_general | solution.py:142
  1088.4 43.2 %all-reduce = (f32[]{:T(128)}, f32[3,3]{1,0:T(4,128)}, f32[256]{0:T(256)}) all-reduce(f32[]{:T(128)S(6)} %mul.987, f32[3,3]{1,0:T(4,128)S(1)} %fusion.82, f32[256]{0:T(256)S(1)} %broadcast_multiply_fusion.1), channel_id=1, replica_groups=mesh['gx'=8,'gy'=4] {'gx','gy'}, use_global_device_ids=true, to_apply=%region_3.4 | all-reduce | flops 266 | bytes 2128 | tf_op jit(solution)/shard_map/psum | solution.py:157
  (415 shorter events, 330.5 us)
Async XLA Ops:
  474.7 5.4 collective-permute-start
  480.2 5.3 collective-permute-start.1
  498.1 53.2 %all-to-all-start = ((f32[1,2,256,2048]{3,1,0,2:T(2,128)}), f32[1,2,256,2048]{3,1,0,2:T(2,128)}, u32[]{:S(2)}, u32[]{:S(2)}) async-start(f32[1,2,256,2048]{3,1,0,2:T(2,128)} %copy.15), calls=%async_computation | async-start | bytes 8388608 | tf_op jit(solution)/shard_map/all_to_all | solution.py:102
  619.6 96.9 %all-to-all-start.1 = ((f32[4,1,262144]{2,1,0:T(1,128)}), f32[4,1,262144]{2,1,0:T(1,128)}, u32[]{:S(2)}, u32[]{:S(2)}) async-start(f32[4,1,262144]{2,1,0:T(1,128)} %reshape.1087), calls=%async_computation.1 | async-start | bytes 8388608 | tf_op jit(solution)/shard_map/all_to_all | solution.py:106
  799.0 2.1 copy-start
  799.0 3.1 copy-start.2
  804.3 1.4 copy-start.1
where the time goes:
time: 1150 us; the launch traced here: 1130 us
  matrix products  403 us (35%)
  local copies, waits for them, and re-layouts  365 us (32%)
  other arithmetic  163 us (14%)
  waiting for transfers between devices  137 us (12%)
  blocking collectives  43.2 us (4%)
  starting transfers between devices  15.2 us (1%)
    dot_general x32, matrix products, shell_rows(): jnp.dot(power_spectrum_row.reshape(-1), onehot, precision=upper_limit)  163 us
    dot_general x16, matrix products, spread(): jnp.einsum('ap,ax->px', factor_yz, factor_x, preferred_element_type=jnp.f...  162 us
    convert_element_type x16, local copies, waits for them, and re-layouts, spread(): factor_yz = (table_y[:, :, None] * wave_table_z[:, None, :]).reshape(bloc...  148 us
    convert_element_type x16, other arithmetic, spread(): factor_yz = (table_y[:, :, None] * wave_table_z[:, None, :]).reshape(bloc...  113 us
    all_to_all x1, waiting for transfers between devices, shards(): lax.all_to_all(along_y.reshape(2, kx_rows, MESH * keep_z)[None], 'gy', sp...  88.8 us
    while x128, local copies, waits for them, and re-layouts  57.7 us
    unnamed x8, local copies, waits for them, and re-layouts  49 us
    all_to_all x1, waiting for transfers between devices, shards(): lax.all_to_all(along_x[None], 'gx', split_axis=2, concat_axis=0, tiled=True)  45.7 us
  transfers between devices with their start and end apart: 4, of which 4 were waited for; matrix products, arithmetic and copies ran while one was open for 1% of the time, Pallas kernels for 0%

commit v1 on v0

--- a/solution.py
+++ b/solution.py
@@ -103,12 +103,18 @@
     moved = moved.reshape(rows_y, 2, kx_rows, keep_y, keep_z)
     table_y = complex_table.reshape(2, 2, MESH, rows_y, plane_y)
     along_y = jnp.einsum("ocKst,scktz->okKz", table_y, moved, precision=upper_limit)
-    shifted_along_z = lax.all_to_all(
-        along_y.reshape(2, kx_rows, MESH * keep_z)[None],
-        "gy",
-        split_axis=3,
-        concat_axis=0,
-        tiled=True,
+    shifted_along_z = jnp.concatenate(
+        lax.all_to_all(
+            jnp.stack(
+                jnp.split(
+                    along_y.reshape(2, kx_rows, MESH * keep_z)[None], lax.axis_size("gy"), axis=3
+                )
+            ),
+            "gy",
+            0,
+            0,
+        ),
+        axis=0,
     )
     shifted_along_z = shifted_along_z.reshape(cols_z, 2, kx_rows, ky_rows, keep_z)
     wave_table_z = complex_table.reshape(2, 2, MESH, cols_z, plane_z)

time: 1150 us -> 1040 us (0.904)
  local copies, waits for them, and re-layouts: 365 us -> 280 us
  other arithmetic: 163 us -> 148 us
    unnamed x8 -> x5, local copies, waits for them, and re-layouts: 49 us -> 4.71 us
    while x128, local copies, waits for them, and re-layouts: 57.7 us -> 30.9 us
    all_to_all x2 -> x1, local copies, waits for them, and re-layouts: 22.6 us -> 6.9 us  [shards(): lax.all_to_all(jnp.stack(jnp.split(along_y.reshape(2, kx_rows, MESH * kee...]
    all_to_all x1 -> x0, other arithmetic: 15.5 us -> none  [shards(): lax.all_to_all(along_y.reshape(2, kx_rows, MESH * keep_z)[None], 'gy', sp...]
where the time goes in v1:
time: 1040 us; the launch traced here: 1030 us
  matrix products  403 us (39%)
  local copies, waits for them, and re-layouts  280 us (27%)
  other arithmetic  148 us (14%)
  waiting for transfers between devices  137 us (13%)
  blocking collectives  43.2 us (4%)
  starting transfers between devices  14.8 us (1%)
    dot_general x32, matrix products, shell_rows(): jnp.dot(power_spectrum_row.reshape(-1), onehot, precision=upper_limit)  163 us
    dot_general x16, matrix products, spread(): jnp.einsum('ap,ax->px', factor_yz, factor_x, preferred_element_type=jnp.f...  162 us
    convert_element_type x16, local copies, waits for them, and re-layouts, spread(): factor_yz = (table_y[:, :, None] * wave_table_z[:, None, :]).reshape(bloc...  149 us
    convert_element_type x16, other arithmetic, spread(): factor_yz = (table_y[:, :, None] * wave_table_z[:, None, :]).reshape(bloc...  113 us
    all_to_all x1, waiting for transfers between devices, shards(): lax.all_to_all(jnp.stack(jnp.split(along_y.reshape(2, kx_rows, MESH * kee...  88.8 us
    all_to_all x1, waiting for transfers between devices, shards(): lax.all_to_all(along_x[None], 'gx', split_axis=2, concat_axis=0, tiled=True)  45.7 us
    dot_general x1, matrix products, shards(): jnp.einsum('akyz,bkyz->ab', vectors * coef[None], vectors, precision=uppe...  45.5 us
    psum x1, blocking collectives, shards(): lax.psum((energy_part, virial_part, spectrum_part), ('gx', 'gy'))  43.2 us
  transfers between devices with their start and end apart: 4, of which 4 were waited for; matrix products, arithmetic and copies ran while one was open for 1% of the time, Pallas kernels for 0%

profile of v1, /device:TPU:14, one launch (start us, length us, event | category | flops | bytes accessed | tf_op | source)
XLA Modules:
  0.0 1030.8 jit_solution(5828784399566122841)
XLA Ops:
  0.6 474.1 %while.31 = (s32[]{:T(128)}, f32[2345,256]{1,0:T(8,128)S(1)}, s32[3,32768]{1,0:T(4,128)}, s32[]{:T(128)}, f32[3,32768]{1,0:T(4,128)}, /*index=5*/s32[]{:T(128)},...) while((s32[]{:T(128)}, f32[2345,256]{1,0:T(8,128)S(1)}, ...), condition=%wide.region_1.2_spmd.clone.clone, body=%wide.region_0.1_spmd.clone.clone.sunk | while | flops 2479059456 | bytes 45443312 | solution.py:85
  3.1 7.1 multiply_convert_fusion.6
  10.1 9.3 convert_element_type.169
  20.2 10.1 convolution_add_fusion.2
  32.7 7.1 multiply_convert_fusion.6
  39.8 9.3 convert_element_type.169
  49.8 10.1 convolution_add_fusion.2
  62.3 7.1 multiply_convert_fusion.6
  69.4 9.3 convert_element_type.169
  79.4 10.1 convolution_add_fusion.2
  91.9 7.1 multiply_convert_fusion.6
  99.0 9.3 convert_element_type.169
  109.1 10.1 convolution_add_fusion.2
  121.6 7.1 multiply_convert_fusion.6
  128.7 9.3 convert_element_type.169
  138.7 10.1 convolution_add_fusion.2
  151.2 7.1 multiply_convert_fusion.6
  158.3 9.3 convert_element_type.169
  168.3 10.1 convolution_add_fusion.2
  180.9 7.1 multiply_convert_fusion.6
  187.9 9.3 convert_element_type.169
  198.0 10.1 convolution_add_fusion.2
  210.5 7.1 multiply_convert_fusion.6
  217.6 9.3 convert_element_type.169
  227.6 10.1 convolution_add_fusion.2
  240.1 7.1 multiply_convert_fusion.6
  247.2 9.3 convert_element_type.169
  257.2 10.1 convolution_add_fusion.2
  269.8 7.1 multiply_convert_fusion.6
  276.8 9.3 convert_element_type.169
  286.9 10.1 convolution_add_fusion.2
  299.4 7.1 multiply_convert_fusion.6
  306.5 9.3 convert_element_type.169
  316.5 10.1 convolution_add_fusion.2
  329.0 7.1 multiply_convert_fusion.6
  336.1 9.3 convert_element_type.169
  346.1 10.1 convolution_add_fusion.2
  358.7 7.1 multiply_convert_fusion.6
  365.7 9.3 convert_element_type.169
  375.8 10.1 convolution_add_fusion.2
  388.3 7.1 multiply_convert_fusion.6
  395.4 9.3 convert_element_type.169
  405.4 10.1 convolution_add_fusion.2
  417.9 7.1 multiply_convert_fusion.6
  425.0 9.3 convert_element_type.169
  435.0 10.1 convolution_add_fusion.2
  447.6 7.1 multiply_convert_fusion.6
  454.6 9.3 convert_element_type.169
  464.7 10.1 convolution_add_fusion.2
  498.2 6.1 all-to-all-start
  505.5 45.7 %all-to-all-done = f32[1,2,256,2048]{3,1,0,2:T(2,128)} async-done(((f32[1,2,256,2048]{3,1,0,2:T(2,128)}), f32[1,2,256,2048]{3,1,0,2:T(2,128)}, u32[]{:S(2)}, u32[]{:S(2)}) %all-to-all-start) | async-done | bytes 4194336 | tf_op jit(solution)/shard_map/all_to_all | solution.py:102
  551.1 8.0 copy.31
  559.1 7.9 reshape.1072
  567.0 17.7 %fusion.64 = f32[2,32,256,64]{2,3,0,1:T(8,128)} fusion(f32[8,2,32,32,64,1]{4,3,0,1,2,5:T(8,128)} %reshape.1072, f32[1,1,256,8,32]{2,4,3,1,0:T(8,128)S(1)} %get-tuple-element.486, f32[1,1,256,8,32]{2,4,3,1,0:T(8,128)S(1)} %get-tuple-element.485, f32[1,1,256,8,32]{2,4,3,1,0:T(8,128)S(1)} %get-tuple-element.484), kind=kOutput, calls=%fused_computation.123 | convolution fusion | flops 6443237376 | bytes 9175040 | tf_op jit(solution)/shard_map/ocKst,scktz->okKz/dot_general | solution.py:105
  584.7 6.9 copy.20
  591.6 7.3 broadcast_in_dim_reshape.3
  603.6 6.8 all-to-all-start.1
  611.7 88.8 %all-to-all-done.1 = f32[4,1,2,32,4096]{4,3,2,1,0:T(8,128)} async-done(((f32[4,1,2,32,4096]{4,3,2,1,0:T(8,128)}), f32[4,1,2,32,4096]{4,3,2,1,0:T(8,128)}, u32[]{:S(2)}, u32[]{:S(2)}) %all-to-all-start.1) | async-done | bytes 4194336 | tf_op jit(solution)/shard_map/all_to_all | solution.py:107
  700.5 6.9 copy.21
  707.4 8.2 reshape.1075
  715.6 9.8 fusion.67
  731.3 196.1 %while.30 = (s32[]{:T(128)}, f32[256]{0:T(256)S(1)}, f32[32,64,256]{2,1,0:T(8,128)S(1)}, s32[32,64,256]{2,1,0:T(8,128)}, s32[]{:T(128)}, /*index=5*/s32[]{:T(128)}) while((s32[]{:T(128)}, f32[256]{0:T(256)S(1)}, f32[32,64,256]{2,1,0:T(8,128)S(1)}, s32[32,64,256]{2,1,0:T(8,128)}, s32[]{:T(128)}, /*index=5*/s32[]{:T(128)}) %tuple.125), condition=%wide.region_6.7_spmd.clone, body=%wide.region_5.6_spmd.clone.sunk | while | flops 54526464 | bytes 659543 | solution.py:161
  937.2 45.5 %fusion.85 = f32[3,3]{1,0:T(4,128)S(1)} fusion(f32[1,32,64,256]{3,0,2,1:T(1,128)} %stack_broadcast_in_dim.8, f32[1,32,64,256]{3,0,2,1:T(1,128)} %stack_broadcast_in_dim.7, f32[1,32,64,256]{3,0,2,1:T(1,128)} %stack_broadcast_in_dim.6, f32[32,64,256]{2,1,0:T(8,128)S(1)} %copy-done.1, f32[]{:T(128)} %multiply_reduce_fusion), kind=kOutput, calls=%fused_computation.135 | convolution fusion | flops 64487460 | bytes 8388648 | tf_op jit(solution)/shard_map/akyz,bkyz->ab/dot_general | solution.py:148
  987.4 43.2 %all-reduce = (f32[]{:T(128)}, f32[3,3]{1,0:T(4,128)}, f32[256]{0:T(256)}) all-reduce(f32[]{:T(128)S(6)} %mul.987, f32[3,3]{1,0:T(4,128)S(1)} %fusion.85, f32[256]{0:T(256)S(1)} %broadcast_multiply_fusion.1), channel_id=1, replica_groups=mesh['gx'=8,'gy'=4] {'gx','gy'}, use_global_device_ids=true, to_apply=%region_3.4 | all-reduce | flops 266 | bytes 2128 | tf_op jit(solution)/shard_map/psum | solution.py:163
  (412 shorter events, 293.9 us)
Async XLA Ops:
  474.9 5.4 collective-permute-start
  480.3 5.2 collective-permute-start.1
  498.2 53.0 %all-to-all-start = ((f32[1,2,256,2048]{3,1,0,2:T(2,128)}), f32[1,2,256,2048]{3,1,0,2:T(2,128)}, u32[]{:S(2)}, u32[]{:S(2)}) async-start(f32[1,2,256,2048]{3,1,0,2:T(2,128)} %copy.18), calls=%async_computation | async-start | bytes 8388608 | tf_op jit(solution)/shard_map/all_to_all | solution.py:102
  603.6 96.9 %all-to-all-start.1 = ((f32[4,1,2,32,4096]{4,3,2,1,0:T(8,128)}), f32[4,1,2,32,4096]{4,3,2,1,0:T(8,128)}, u32[]{:S(2)}, u32[]{:S(2)}) async-start(f32[4,1,2,32,4096]{4,3,2,1,0:T(8,128)} %pad_maximum_fusion), calls=%async_computation.1 | async-start | bytes 8388608 | tf_op jit(solution)/shard_map/all_to_all | solution.py:107
  715.6 9.8 copy-start
  930.7 6.6 copy-start.1
